TPU v7x, 512 devices: a 4x2x32 block of a 4x16x32 slice. The times are simulated.
512 devices in a mesh: sweep: 2 (over y), expert: 64 (over z, core), dp: 4 (over x).
Axes of the slice: x: 4, y: 2, z: 32, core: 2. Of those that a mesh axis runs over, the one named last changes fastest.
The devices are a block of a 4x16x32 slice.
Arguments:
- tokens: bfloat16 [65536, 1536], P(('sweep', 'expert', 'dp')), parts along dimension 0, may hold values from -6 to 6
- expert_ids: int32 [65536, 8], P(('sweep', 'expert', 'dp')), parts along dimension 0, may hold values from 0 to 63, all different within a row; in each aligned block of 128 rows (0 to 127, 128 to 255, ...) at most 20 rows name the same one
- gate_weights: float32 [65536, 8], P(('sweep', 'expert', 'dp')), parts along dimension 0, may hold values from 0.1 to 0.6
- expert_in: bfloat16 [128, 1536, 768], P(('sweep', 'expert'), 'dp'), parts along dimension 0, may hold values from -0.15625 to 0.15625
- expert_out: bfloat16 [128, 768, 1536], P(('sweep', 'expert'), None, 'dp'), parts along dimension 0, may hold values from -0.21875 to 0.21875
- shared_in: bfloat16 [3072, 768], P(('sweep', 'dp')), parts along dimension 0, may hold values from -0.15625 to 0.15625
- shared_out: bfloat16 [1536, 1536], P('sweep', 'dp'), parts along dimension 0, may hold values from -0.21875 to 0.21875
Outputs:
- block_out: bfloat16 [65536, 1536], P(('sweep', 'expert', 'dp')), parts along dimension 0
There are 2 independent parts, one for each index of `sweep`. A program takes and returns all parts, laid end to end along the dimension named above; each array names one. Nothing has to cross between parts.
Inputs may be any that keep to these rules, and one draw needn't show every extreme that they name: `expert_ids`: each token names 8 different experts. In each aligned block of 128 tokens (the tokens of one device) no expert is named by more than 20 tokens; some blocks have an expert named by exactly 20.
All inputs are finite; a program needn't handle non-finite values.
Results may differ from a plain program's by a relative error of at most 0.0051.
Values may be sent and summed in bfloat16 or wider, within the bound.
A program may use at most 64 MiB of HBM per device.

v0:
```python
import jax
import jax.numpy as jnp
from jax import lax
from jax.sharding import PartitionSpec as P

CAP = 20


def layer_norm(tokens):
    values = tokens.astype(jnp.float32)
    center = values - jnp.mean(values, axis=-1, keepdims=True)
    spread = jnp.mean(center * center, axis=-1, keepdims=True)
    return (center * lax.rsqrt(spread + 1e-06)).astype(jnp.bfloat16)


def copy_slots(expert_ids, expert_count):
    expert_iota = jnp.arange(expert_count, dtype=jnp.int32)
    matches = (expert_ids[..., None] == expert_iota).astype(jnp.int32)
    per_token = jnp.sum(matches, axis=-2, dtype=jnp.int32)
    earlier = jnp.cumsum(per_token, axis=-2, dtype=jnp.int32) - per_token
    return jnp.sum(matches * earlier[..., None, :], axis=-1, dtype=jnp.int32)


def run_experts(shard_piece, weight_in, weight_out):
    pre_act = jnp.einsum(
        "gesd,edf->gesf", shard_piece, weight_in, preferred_element_type=jnp.float32
    )
    hidden = jax.nn.gelu(pre_act).astype(jnp.bfloat16)
    return jnp.einsum(
        "gesf,efd->gesd", hidden, weight_out, preferred_element_type=jnp.float32
    ).astype(jnp.bfloat16)


def per_device(tokens, expert_ids, gate_weights, expert_in, expert_out, shared_in, shared_out):
    row_count, model_width = tokens.shape
    pick_count = expert_ids.shape[1]
    local_count = expert_in.shape[0]
    group_count = lax.axis_size("expert")
    expert_total = local_count * group_count
    normed = layer_norm(tokens)
    full_in, full_out, shared_full_in, shared_full_out = (
        lax.all_gather(expert_in, "dp", axis=1, tiled=True),
        lax.all_gather(expert_out, "dp", axis=2, tiled=True),
        lax.all_gather(shared_in, "dp", axis=0, tiled=True),
        lax.all_gather(shared_out, "dp", axis=1, tiled=True),
    )
    slot_of = copy_slots(expert_ids, expert_total)
    positions = (expert_ids * CAP + slot_of).reshape(-1)
    copies = jnp.repeat(normed, pick_count, axis=0)
    outgoing = jnp.zeros((expert_total * CAP, model_width), jnp.bfloat16).at[positions].set(copies)
    outgoing = outgoing.reshape(group_count, local_count, CAP, model_width)
    received = lax.all_to_all(outgoing, "expert", split_axis=0, concat_axis=0, tiled=True)
    returned = lax.all_to_all(
        run_experts(received, full_in, full_out), "expert", split_axis=0, concat_axis=0, tiled=True
    )
    results = returned.reshape(expert_total * CAP, model_width)[positions].reshape(
        row_count, pick_count, model_width
    )
    routed = jnp.sum(results.astype(jnp.float32) * gate_weights[:, :, None], axis=1)
    shared_pre = jnp.dot(normed, shared_full_in, preferred_element_type=jnp.float32)
    shared_hidden = jax.nn.gelu(shared_pre).astype(jnp.bfloat16)
    shared_result = jnp.dot(shared_hidden, shared_full_out, preferred_element_type=jnp.float32)
    return (tokens.astype(jnp.float32) + shared_result + routed).astype(jnp.bfloat16)


def solution(mesh):
    placed = (
        P(("sweep", "expert", "dp"), None),
        P(("sweep", "expert", "dp"), None),
        P(("sweep", "expert", "dp"), None),
        P(("sweep", "expert"), "dp", None),
        P(("sweep", "expert"), None, "dp"),
        P(("sweep", "dp"), None),
        P("sweep", "dp"),
    )
    return jax.shard_map(
        per_device,
        mesh=mesh,
        in_specs=placed,
        out_specs=P(("sweep", "expert", "dp"), None),
        check_vma=False,
    )
```

profile of v0, /device:TPU:40, one launch (start us, length us, event | category | flops | bytes accessed | tf_op | source)
XLA Modules:
  0.0 981.0 jit_solution(12768818425173448620)
XLA Ops:
  6.5 1.1 convert_reduce_fusion
  7.7 1.2 fusion.36
  8.9 1.2 fusion.37
  10.2 0.7 convert_reduce_fusion.1
  10.9 0.1 copy.21
  11.0 0.2 reduce_window_sum.11
  11.2 0.1 copy.23
  11.3 0.7 select_reduce_fusion
  12.0 0.7 multiply_add_fusion
  12.7 0.1 copy.24
  12.8 0.1 reshape.81
  12.9 7.9 scatter_custom_fusion
  20.8 6.9 reshape.83
  27.7 47.4 %all-to-all-start = ((bf16[64,1,20,1536]{3,2,1,0:T(8,128)(2,1)}), bf16[64,1,20,1536]{3,2,1,0:T(8,128)(2,1)}, u32[]{:S(2)}, u32[]{:S(2)}) async-start(bf16[64,1,20,1536]{3,2,1,0:T(8,128)(2,1)} %bitcast.48), calls=%async_computation | async-start | bytes 9437184 | tf_op jit(solution)/shard_map/all_to_all | solution.py:52
  75.1 0.1 all-gather.11.cloned.1.call-start
  75.1 0.7 all-gather.11.cloned.1.call-update
  75.9 0.2 all-gather.9.cloned.1.call-start
  76.1 0.6 all-gather.9.cloned.1.call-update
  76.7 50.6 %all-gather.11.cloned.1.call-done = bf16[1,768,1536]{2,1,0:T(8,128)(2,1)} async-done(((bf16[1,768,384]{2,1,0:T(8,128)(2,1)}), bf16[1,768,1536]{2,1,0:T(8,128)(2,1)}) %all-gather.11.cloned.1.call-update) | async-done | bytes 2359312 | tf_op jit(solution)/shard_map/all_gather | solution.py:43
  127.2 51.5 %all-gather.9.cloned.1.call-done = bf16[1,1536,768]{2,1,0:T(8,128)(2,1)} async-done(((bf16[1,384,768]{2,1,0:T(8,128)(2,1)}), bf16[1,1536,768]{2,1,0:T(8,128)(2,1)}) %all-gather.9.cloned.1.call-update) | async-done | bytes 2359312 | tf_op jit(solution)/shard_map/all_gather | solution.py:42
  178.7 320.2 %all-to-all-done = bf16[64,1,20,1536]{3,2,1,0:T(8,128)(2,1)} async-done(((bf16[64,1,20,1536]{3,2,1,0:T(8,128)(2,1)}), bf16[64,1,20,1536]{3,2,1,0:T(8,128)(2,1)}, u32[]{:S(2)}, u32[]{:S(2)}) %all-to-all-start) | async-done | bytes 3932192 | tf_op jit(solution)/shard_map/all_to_all | solution.py:52
  498.9 12.4 %fusion.12 = bf16[64,1,20,1536]{3,0,2,1:T(8,128)(2,1)} fusion(bf16[1,768,1536]{2,1,0:T(8,128)(2,1)} %all-gather.11.cloned.1.call-done, bf16[64,1,20,1536]{3,2,1,0:T(8,128)(2,1)} %all-to-all-done, bf16[1,1536,768]{2,1,0:T(8,128)(2,1)} %all-gather.9.cloned.1.call-done), kind=kOutput, calls=%fused_computation.17 | convolution fusion | flops 6050611200 | bytes 12582912 | tf_op jit(solution)/shard_map/gesf,efd->gesd/dot_general | solution.py:29
  511.3 6.5 copy.27
  517.8 0.0 copy-start.1
  517.8 7.5 all-to-all-start.1
  525.3 0.1 all-gather.5.cloned.1.call-start
  525.4 0.7 all-gather.5.cloned.1.call-update
  526.1 0.3 all-gather.7.cloned.1.call-start
  526.4 0.3 all-gather.7.cloned.1.call-update
  526.8 0.0 copy-done.1
  526.8 0.7 copy.28
  527.5 421.7 %all-to-all-done.1 = bf16[64,1,20,1536]{3,2,1,0:T(8,128)(2,1)} async-done(((bf16[64,1,20,1536]{3,2,1,0:T(8,128)(2,1)}), bf16[64,1,20,1536]{3,2,1,0:T(8,128)(2,1)}, u32[]{:S(2)}, u32[]{:S(2)}) %all-to-all-start.1) | async-done | bytes 3932192 | tf_op jit(solution)/shard_map/all_to_all | solution.py:53
  949.2 6.9 reshape.88
  956.1 9.3 gather_fusion
  965.4 0.0 copy-start
  965.4 4.6 fusion
  970.0 0.0 all-gather.5.cloned.1.call-done
  970.0 0.0 all-gather.7.cloned.1.call-done
  970.0 0.0 copy-done
  970.0 4.4 fusion.16
  (5 shorter events, 0.0 us)
Async XLA Ops:
  27.7 471.2 %all-to-all-start = ((bf16[64,1,20,1536]{3,2,1,0:T(8,128)(2,1)}), bf16[64,1,20,1536]{3,2,1,0:T(8,128)(2,1)}, u32[]{:S(2)}, u32[]{:S(2)}) async-start(bf16[64,1,20,1536]{3,2,1,0:T(8,128)(2,1)} %bitcast.48), calls=%async_computation | async-start | bytes 9437184 | tf_op jit(solution)/shard_map/all_to_all | solution.py:52
  75.1 52.2 %all-gather.11.cloned.1.call-start = ((), (), s32[]{:S(2)}) async-start(), calls=%async_computation.5 | async-start | bytes 2949120 | tf_op jit(solution)/shard_map/all_gather | solution.py:43
  75.9 102.8 %all-gather.9.cloned.1.call-start = ((), (), s32[]{:S(2)}) async-start(), calls=%async_computation.4 | async-start | bytes 2949120 | tf_op jit(solution)/shard_map/all_gather | solution.py:42
  517.8 8.9 copy-start.1
  517.8 431.4 %all-to-all-start.1 = ((bf16[64,1,20,1536]{3,2,1,0:T(8,128)(2,1)}), bf16[64,1,20,1536]{3,2,1,0:T(8,128)(2,1)}, u32[]{:S(2)}, u32[]{:S(2)}) async-start(bf16[64,1,20,1536]{3,2,1,0:T(8,128)(2,1)} %copy.27), calls=%async_computation.1 | async-start | bytes 9437184 | tf_op jit(solution)/shard_map/all_to_all | solution.py:53
  525.3 444.7 %all-gather.5.cloned.1.call-start = ((), (), s32[]{:S(2)}) async-start(), calls=%async_computation.2 | async-start | bytes 2949120 | tf_op jit(solution)/shard_map/all_gather | solution.py:44
  526.1 443.9 %all-gather.7.cloned.1.call-start = ((), (), s32[]{:S(2)}) async-start(), calls=%async_computation.3 | async-start | bytes 2949120 | tf_op jit(solution)/shard_map/all_gather | solution.py:45
  965.4 4.6 copy-start
Sparse Core Ops, SparseCore 0:
  78.1 49.1 all-gather.10
  129.4 49.3 all-gather.8
  528.3 49.1 all-gather.4
  579.5 49.2 all-gather.6
where the time goes:
time: 982 us; the launch traced here: 981 us
  waiting for transfers between devices  846 us (86%)
  starting transfers between devices  55.5 us (6%)
  local copies, waits for them, and re-layouts  38.6 us (4%)
  matrix products  16.8 us (2%)
  between operations  13.2 us (1%)
  other arithmetic  10.5 us (1%)
    all_to_all x1, waiting for transfers between devices, per_device(): lax.all_to_all(run_experts(received, full_in, full_out), 'expert', split_...  422 us
    all_to_all x1, waiting for transfers between devices, per_device(): lax.all_to_all(outgoing, 'expert', split_axis=0, concat_axis=0, tiled=True)  320 us
    all_gather x1, waiting for transfers between devices, per_device(): lax.all_gather(expert_in, 'dp', axis=1, tiled=True)  51.5 us
    all_gather x1, waiting for transfers between devices, per_device(): lax.all_gather(expert_out, 'dp', axis=2, tiled=True)  50.6 us
    all_to_all x1, starting transfers between devices, per_device(): lax.all_to_all(outgoing, 'expert', split_axis=0, concat_axis=0, tiled=True)  47.4 us
  transfers between devices with their start and end apart: 6, of which 4 were waited for; matrix products, arithmetic and copies ran while one was open for 2% of the time, Pallas kernels for 0%

commit v1 on v0

v1 whole, which is shorter than its diff:
```python
import functools

import jax
import jax.numpy as jnp
from jax import lax
from jax.experimental import pallas as pl
from jax.experimental.pallas import tpu as pltpu
from jax.sharding import PartitionSpec as P

CORES = 2
SLOTS = 32
CHUNKS = 4
FFN_FROM = 7
MESH = pl.DeviceIdType.MESH


def kernel(
    chips, dp, tok_ref, meta_ref, win_ref, wout_ref, sin_ref, sout_ref, out_ref,
    db, mb, st, xb, xs, rc, rs, rb, hb, base, win, wout, sin, sout,
    d_recv, d_send, m_recv, m_send, x_recv, x_send, r_recv, r_send, a_recv, a_send,
    w_recv, w_send, w_loc,
):
    far_r = chips // 2
    far_l = chips - 1 - far_r
    own = far_r - 1
    rows, width = tok_ref.shape
    hidden = win.shape[1]
    part = rows // CHUNKS
    me = lax.axis_index("expert")
    core = lax.rem(me, CORES)
    chip = me // CORES
    right = lax.rem(chip + 1, chips) * CORES + core
    left = lax.rem(chip + chips - 1, chips) * CORES + core
    partner = chip * CORES + (1 - core)
    xi = lax.axis_index("dp")
    x_up, x_down = lax.rem(xi + 1, dp), lax.rem(xi + dp - 1, dp)
    towards = (right, left)

    barrier = pltpu.get_barrier_semaphore()
    for peer in ({"expert": right}, {"expert": left}, {"expert": partner}, {"dp": x_up}, {"dp": x_down}):
        pl.semaphore_signal(barrier, inc=1, device_id=peer, device_id_type=MESH)

    def norm_rows(i, carry):
        rows_i = pl.ds(i * 16, 16)
        values = tok_ref[rows_i, :].astype(jnp.float32)
        center = values - jnp.mean(values, axis=-1, keepdims=True)
        spread = jnp.mean(center * center, axis=-1, keepdims=True)
        db[1, own, rows_i, :] = (center * lax.rsqrt(spread + 1e-06)).astype(jnp.bfloat16)
        return carry

    lax.fori_loop(0, rows // 16, norm_rows, 0)
    mb[1, own] = meta_ref[...]
    pl.semaphore_wait(barrier, 5)

    def piece(k):
        return pl.ds(k * part, part)

    def block_copy(way, source, arrive, k):
        return pltpu.make_async_remote_copy(
            src_ref=db.at[source[0], source[1], piece(k)],
            dst_ref=db.at[way, arrive, piece(k)],
            send_sem=d_send.at[way, arrive],
            recv_sem=d_recv.at[way, arrive, k],
            device_id={"expert": towards[way]},
            device_id_type=MESH,
        )

    def meta_copy(way, source, arrive):
        return pltpu.make_async_remote_copy(
            src_ref=mb.at[source[0], source[1]],
            dst_ref=mb.at[way, arrive],
            send_sem=m_send.at[way, arrive],
            recv_sem=m_recv.at[way, arrive],
            device_id={"expert": towards[way]},
            device_id_type=MESH,
        )

    for way in (0, 1):
        meta_copy(way, (1, own), 0).start()
    for k in range(CHUNKS):
        for way in (0, 1):
            block_copy(way, (1, own), 0, k).start()

    d_part, f_part = win_ref.shape[1], wout_ref.shape[2]

    def region(a, shard):
        if a in (0, 2):
            return (win, sin)[a // 2].at[pl.ds(shard * d_part, d_part), :]
        return (wout, sout)[a // 2].at[:, pl.ds(pl.multiple_of(shard * f_part, 128), f_part)]

    shards = (win_ref.at[0], wout_ref.at[0], sin_ref, sout_ref)

    def weight_copy(a, k):
        shard = lax.rem(xi + dp - k, dp) if a in (0, 2) else lax.rem(xi + k, dp)
        return pltpu.make_async_remote_copy(
            src_ref=shards[a] if k == 0 else region(a, shard),
            dst_ref=region(a, shard),
            send_sem=w_send.at[a, k],
            recv_sem=w_recv.at[a, k],
            device_id={"dp": x_up if a in (0, 2) else x_down},
            device_id_type=MESH,
        )

    def local_copy(a):
        return pltpu.make_async_copy(shards[a], region(a, xi), w_loc.at[a])

    for a in range(4):
        local_copy(a).start()
    for a in (0, 1):
        weight_copy(a, 0).start()

    def slot_copy(way, at):
        return pltpu.make_async_remote_copy(
            src_ref=xs.at[at, way],
            dst_ref=xb.at[at, pl.ds(way * 2 * SLOTS + SLOTS, SLOTS)],
            send_sem=x_send.at[way, at],
            recv_sem=x_recv.at[way, at],
            device_id={"expert": partner},
            device_id_type=MESH,
        )

    def result_copy(way, at):
        return pltpu.make_async_remote_copy(
            src_ref=rs.at[at, way],
            dst_ref=rc.at[at, way, pl.ds(SLOTS, SLOTS)],
            send_sem=r_send.at[way, at],
            recv_sem=r_recv.at[way, at],
            device_id={"expert": partner},
            device_id_type=MESH,
        )

    def sum_copy(way, step, k):
        return pltpu.make_async_remote_copy(
            src_ref=rb.at[way, step, piece(k)],
            dst_ref=rb.at[way, step + 1, piece(k)],
            send_sem=a_send.at[way, step],
            recv_sem=a_recv.at[way, step + 1, k],
            device_id={"expert": towards[1 - way]},
            device_id_type=MESH,
        )

    def gather(way, at):
        ids = mb[way, at, 0:8, :]
        gates = mb[way, at, 8:16, :]
        match, gate = [], []
        for expert in (me, partner):
            hit = ids == expert.astype(jnp.float32)
            match.append(jnp.sum(jnp.where(hit, 1.0, 0.0), axis=0, keepdims=True))
            gate.append(jnp.sum(jnp.where(hit, gates, 0.0), axis=0, keepdims=True))
        both = jnp.concatenate([jnp.broadcast_to(m, (8, rows)) for m in match], axis=0)
        before = lax.broadcasted_iota(jnp.int32, (rows, rows), 0) < lax.broadcasted_iota(jnp.int32, (rows, rows), 1)
        earlier = jnp.dot(
            both.astype(jnp.bfloat16),
            jnp.where(before, 1.0, 0.0).astype(jnp.bfloat16),
            preferred_element_type=jnp.float32,
        )
        slot = jnp.where(both > 0.5, earlier, -1.0)
        row = lax.broadcasted_iota(jnp.int32, (SLOTS, rows), 0).astype(jnp.float32)
        pick, spread = [], []
        for i in (0, 1):
            here = jnp.concatenate([slot[8 * i : 8 * i + 8]] * (SLOTS // 8), axis=0) == row
            pick.append(jnp.where(here, 1.0, 0.0))
            spread.append(jnp.where(here, jnp.broadcast_to(gate[i], (SLOTS, rows)), 0.0))
        picked = jnp.concatenate(pick, axis=0).astype(jnp.bfloat16)
        st[way, at] = jnp.concatenate(spread, axis=0).T.astype(jnp.bfloat16)
        tile = 256
        for n in range(width // tile):
            cols = pl.ds(n * tile, tile)
            got = jnp.dot(picked, db[way, at, :, cols], preferred_element_type=jnp.float32).astype(jnp.bfloat16)
            xb[at, pl.ds(way * 2 * SLOTS, SLOTS), cols] = got[:SLOTS]
            xs[at, way, :, cols] = got[SLOTS:]
        slot_copy(way, at).start()

    def two_dots(source, first, second, store):
        tile = 256
        for n in range(hidden // tile):
            cols = pl.ds(n * tile, tile)
            pre = jnp.dot(source(), first[:, cols], preferred_element_type=jnp.float32)
            hb[:, cols] = jax.nn.gelu(pre, approximate=True).astype(jnp.bfloat16)
        for n in range(width // tile):
            cols = pl.ds(n * tile, tile)
            store(cols, jnp.dot(hb[...], second[:, cols], preferred_element_type=jnp.float32))

    def ffn(at):
        for way in (0, 1):
            slot_copy(way, at).wait_recv()

        def store(cols, result):
            result = result.astype(jnp.bfloat16)
            for way in (0, 1):
                lo = way * 2 * SLOTS
                rc[at, way, pl.ds(0, SLOTS), cols] = result[lo : lo + SLOTS]
                rs[at, way, :, cols] = result[lo + SLOTS : lo + 2 * SLOTS]

        two_dots(lambda: xb[at], win, wout, store)
        for way in (0, 1):
            result_copy(way, at).start()

    def shared_ffn():
        def store(cols, result):
            base[:, cols] = tok_ref[:, cols].astype(jnp.float32) + result

        two_dots(lambda: db[1, own], sin, sout, store)

    def dispatch(i, carry):
        step = i + 1

        for k in range(CHUNKS):
            block_copy(0, (0, i), i, k).wait_recv()

            @pl.when(step < far_r)
            def _():
                block_copy(0, (0, i), step, k).start()

            @pl.when(step <= far_l)
            def _():
                block_copy(1, (1, i), i, k).wait_recv()

            @pl.when(step < far_l)
            def _():
                block_copy(1, (1, i), step, k).start()

            if k == 0:
                meta_copy(0, (0, i), i).wait_recv()

                @pl.when(step < far_r)
                def _():
                    meta_copy(0, (0, i), step).start()

                @pl.when(step <= far_l)
                def _():
                    meta_copy(1, (1, i), i).wait_recv()

                @pl.when(step < far_l)
                def _():
                    meta_copy(1, (1, i), step).start()

                @pl.when(step == 1)
                def _():
                    gather(1, own)

                @pl.when(step > 1)
                def _():
                    gather(0, i - 1)

            if k == 1:

                @pl.when(step > 1)
                def _():
                    gather(1, i - 1)

            if k == 2:

                @pl.when(step >= FFN_FROM)
                def _():
                    ffn(i - 2)

            if k == 3:
                for hop in range(dp - 1):
                    for first, pair in ((0, (0, 1)), (2 * dp - 2, (2, 3))):

                        @pl.when(step == min(first + 2 * (hop + 1), far_r))
                        def _():
                            for a in pair:
                                weight_copy(a, hop).wait_recv()
                                if hop + 1 < dp - 1:
                                    weight_copy(a, hop + 1).start()
                                if hop == dp - 2:
                                    local_copy(a).wait()
                                    if a < 2:
                                        weight_copy(a + 2, 0).start()

        return carry

    lax.fori_loop(0, far_r, dispatch, 0)
    gather(0, far_r - 1)
    late = max(0, min(FFN_FROM - 3, far_r - 2))

    def last_units(i, carry):
        ffn(far_r - 2 + i)
        return carry

    lax.fori_loop(0, 2, last_units, 0)

    def combine(way, at, step, k, first):
        at_rows = piece(k)
        total = jnp.dot(st[way, at, at_rows, :], rc[at, way], preferred_element_type=jnp.float32)
        if not first:
            total = total + rb[way, step, at_rows, :].astype(jnp.float32)
        rb[way, step, at_rows, :] = total.astype(jnp.bfloat16)

    for way, far in ((1, far_l), (0, far_r)):
        result_copy(way, far - 1).wait_recv()
        for k in range(CHUNKS):
            combine(way, far - 1, 0, k, True)
        for k in range(CHUNKS):
            sum_copy(way, 0, k).start()

    def bring_back(r, carry):
        for k in range(CHUNKS):
            for way, far in ((0, far_r), (1, far_l)):

                @pl.when(r < far)
                def _():
                    if k == 0:
                        result_copy(way, far - 1 - r).wait_recv()
                    sum_copy(way, r - 1, k).wait_recv()
                    combine(way, far - 1 - r, r, k, False)
                    sum_copy(way, r, k).start()

            if k == 1:

                @pl.when(r <= late)
                def _():
                    ffn(late - r)

            if k == 2:

                @pl.when(r == min(8, far_r - 1))
                def _():
                    shared_ffn()

        return carry

    lax.fori_loop(1, far_r, bring_back, 0)

    result_copy(1, own).wait_recv()
    for k in range(CHUNKS):
        at_rows = piece(k)
        total = base[at_rows, :] + jnp.dot(
            st[1, own, at_rows, :], rc[own, 1], preferred_element_type=jnp.float32
        )
        for way, far in ((1, far_l), (0, far_r)):
            sum_copy(way, far - 1, k).wait_recv()
            total = total + rb[way, far, at_rows, :].astype(jnp.float32)
        out_ref[at_rows, :] = total.astype(jnp.bfloat16)

    def whole(ref, sem):
        return pltpu.make_async_copy(ref, ref, sem)

    for way, far in ((0, far_r), (1, far_l)):

        def drain(i, carry):
            whole(db.at[way, i], d_send.at[way, i]).wait()
            whole(mb.at[way, i], m_send.at[way, i]).wait()
            whole(rb.at[way, i], a_send.at[way, i]).wait()
            return carry

        lax.fori_loop(0, far, drain, 0)

        def drain_pair(i, carry):
            slot_copy(way, i).wait_send()
            result_copy(way, i).wait_send()
            return carry

        lax.fori_loop(0, far_r, drain_pair, 0)
    for a in range(4):
        for k in range(dp - 1):
            weight_copy(a, k).wait_send()


def per_device(mesh, tokens, expert_ids, gate_weights, expert_in, expert_out, shared_in, shared_out):
    rows, width = tokens.shape
    hidden = expert_in.shape[2]
    chips, dp = mesh.shape["expert"] // CORES, mesh.shape["dp"]
    far = chips // 2
    meta = jnp.concatenate([expert_ids.astype(jnp.float32).T, gate_weights.T], axis=0)
    vmem = pl.BlockSpec(memory_space=pltpu.VMEM)
    hbm = pl.BlockSpec(memory_space=pl.ANY)
    b16, f32, dma = jnp.bfloat16, jnp.float32, pltpu.SemaphoreType.DMA
    return pl.pallas_call(
        functools.partial(kernel, chips, dp),
        out_shape=jax.ShapeDtypeStruct((rows, width), b16),
        in_specs=[vmem, vmem, hbm, hbm, hbm, hbm],
        out_specs=vmem,
        scratch_shapes=[
            pltpu.VMEM((2, far, rows, width), b16),
            pltpu.VMEM((2, far, 16, rows), f32),
            pltpu.VMEM((2, far, rows, 2 * SLOTS), b16),
            pltpu.VMEM((far, 4 * SLOTS, width), b16),
            pltpu.VMEM((far, 2, SLOTS, width), b16),
            pltpu.VMEM((far, 2, 2 * SLOTS, width), b16),
            pltpu.VMEM((far, 2, SLOTS, width), b16),
            pltpu.VMEM((2, far + 1, rows, width), b16),
            pltpu.VMEM((rows, hidden), b16),
            pltpu.VMEM((rows, width), f32),
            pltpu.VMEM((width, hidden), b16),
            pltpu.VMEM((hidden, width), b16),
            pltpu.VMEM((width, hidden), b16),
            pltpu.VMEM((hidden, width), b16),
            dma((2, far, CHUNKS)),
            dma((2, far)),
            dma((2, far)),
            dma((2, far)),
            dma((2, far)),
            dma((2, far)),
            dma((2, far)),
            dma((2, far)),
            dma((2, far + 1, CHUNKS)),
            dma((2, far)),
            dma((4, dp - 1)),
            dma((4, dp - 1)),
            dma((4,)),
        ],
        compiler_params=pltpu.CompilerParams(
            collective_id=0, has_side_effects=True, vmem_limit_bytes=67043328
        ),
        name="moe_ring",
    )(tokens, meta, expert_in, expert_out, shared_in, shared_out)


def solution(mesh):
    placed = (
        P(("sweep", "expert", "dp"), None),
        P(("sweep", "expert", "dp"), None),
        P(("sweep", "expert", "dp"), None),
        P(("sweep", "expert"), "dp", None),
        P(("sweep", "expert"), None, "dp"),
        P(("sweep", "dp"), None),
        P("sweep", "dp"),
    )
    return jax.shard_map(
        functools.partial(per_device, mesh),
        mesh=mesh,
        in_specs=placed,
        out_specs=P(("sweep", "expert", "dp"), None),
        check_vma=False,
    )
```

time: 982 us -> 336 us (0.34)
  waiting for transfers between devices: 846 us -> 0 us
  Pallas kernels: 0 us -> 332 us
  starting transfers between devices: 55.5 us -> 0 us
  local copies, waits for them, and re-layouts: 38.6 us -> 1.77 us
  matrix products: 16.8 us -> 0 us
  between operations: 13.2 us -> 0.01 us
    all_to_all x2 -> x0, waiting for transfers between devices: 742 us -> none  [the longest x1 422 us: per_device(): lax.all_to_all(run_experts(received, full_in, full_out), 'expert', split_...]
    pallas_call x0 -> x1, Pallas kernels: none -> 332 us  [per_device(): pl.pallas_call(functools.partial(kernel, chips, dp), out_shape=jax.ShapeD...]
    all_gather x4 -> x0, waiting for transfers between devices: 102 us -> none  [the longest x1 51.5 us: per_device(): lax.all_gather(expert_in, 'dp', axis=1, tiled=True)]
    all_to_all x2 -> x0, starting transfers between devices: 54.8 us -> none  [the longest x1 47.4 us: per_device(): lax.all_to_all(outgoing, 'expert', split_axis=0, concat_axis=0, tiled=True)]
    dot_general x2 -> x0, matrix products: 16.8 us -> none  [the longest x1 12.4 us: run_experts(): jnp.einsum('gesf,efd->gesd', hidden, weight_out, preferred_element_type=j...]
    reshape x3 -> x0, local copies, waits for them, and re-layouts: 13.9 us -> none  [the longest x1 6.92 us: per_device(): returned.reshape(expert_total * CAP, model_width)[positions]]
  transfers between devices with their start and end apart: 6 -> 0, of which waited for: 4 -> 0; matrix products, arithmetic and copies ran while one was open for 2% -> 0% of each run, Pallas kernels for 0% -> 0%
where the time goes in v1:
time: 336 us; the launch traced here: 335 us
  Pallas kernels  332 us (99%)
    pallas_call x1, Pallas kernels, per_device(): pl.pallas_call(functools.partial(kernel, chips, dp), out_shape=jax.ShapeD...  332 us

profile of v1, /device:TPU:40, one launch (start us, length us, event | category | flops | bytes accessed | tf_op | source)
XLA Modules:
  0.0 334.9 jit_solution(18009421744760190863)
XLA Ops:
  0.0 0.0 copy-start
  0.0 0.7 convert_bitcast_fusion
  0.7 0.0 copy-done
  0.7 0.6 pad_maximum_fusion.meta_ref
  1.3 331.8 %moe_ring.1 = bf16[128,1536]{1,0:T(8,128)(2,1)} custom-call(bf16[128,1536]{1,0:T(8,128)(2,1)} %tok_ref.1, f32[16,128]{1,0:T(8,128)} %pad_maximum_fusion.meta_ref, bf16[1,384,768]{2,1,0:T(8,128)(2,1)} %win_ref.1, bf16[1,768,384]{2,1,0:T(8,128)(2,1)} %wout_ref.1, bf16[384,768]{1,0:T(8,128)(2,1)} %sin_ref.1, bf16[768,384]{1,0:T(8,128)(2,1)} %sout_ref.1), custom_call_target="tpu_custom_call" | custom-call | tf_op jit(solution)/shard_map/moe_ring/pallas_call | solution.py:371
  333.1 1.8 copy.9
Async XLA Ops:
  0.0 0.7 copy-start

commit v2 on v0

v2 whole, which is shorter than its diff:
```python
import functools

import jax
import jax.numpy as jnp
from jax import lax
from jax.experimental import pallas as pl
from jax.experimental.pallas import tpu as pltpu
from jax.sharding import PartitionSpec as P

CORES = 2
SLOTS = 32
PACK = 64
CHUNKS = 4
FFN_FROM = 8
STAGGER = 3
TILE = 256
MESH = pl.DeviceIdType.MESH


def kernel(
    chips, dp, tok_ref, meta_ref, win_ref, wout_ref, sin_ref, sout_ref, out_ref,
    nb, db, mb, st, sp, pq, pin, xb, rc, r16, rq, rp, rb, hb, base, win, wout, sin, sout,
    d_recv, d_send, m_recv, m_send, q_recv, q_send, f_recv, f_send,
    e_recv, e_send, g_recv, g_send, a_recv, a_send,
    w_recv, w_send, w_loc, p_recv, p_send, go,
):
    far = chips // 2
    full = far - 2
    pairs = far // 2
    rows, width = tok_ref.shape
    hidden = win.shape[2]
    part = rows // CHUNKS
    me = lax.axis_index("expert")
    core = lax.rem(me, CORES)
    chip = me // CORES
    right = lax.rem(chip + 1, chips) * CORES + core
    left = lax.rem(chip + chips - 1, chips) * CORES + core
    partner = chip * CORES + (1 - core)
    xi = lax.axis_index("dp")
    x_up, x_down = lax.rem(xi + 1, dp), lax.rem(xi + dp - 1, dp)
    towards = (right, left)

    barrier = pltpu.get_barrier_semaphore()
    for peer in ({"expert": right}, {"expert": left}, {"expert": partner}, {"dp": x_up}, {"dp": x_down}):
        pl.semaphore_signal(barrier, inc=1, device_id=peer, device_id_type=MESH)

    def remote(source, target, send, recv, device):
        return pltpu.make_async_remote_copy(
            src_ref=source, dst_ref=target, send_sem=send, recv_sem=recv,
            device_id=device, device_id_type=MESH,
        )

    def to(way):
        return {"expert": towards[way]}

    def piece(k):
        return pl.ds(k * part, part)

    def own_copy(way, k):
        return remote(nb.at[piece(k)], db.at[way, 0, piece(k)], d_send.at[way, 0], d_recv.at[way, 0, k], to(way))

    def block_copy(way, at, k):
        return remote(
            db.at[way, at, piece(k)], db.at[way, at + 1, piece(k)], d_send.at[way, at + 1], d_recv.at[way, at + 1, k], to(way)
        )

    def arrived(way, at, k):
        spot = db.at[way, at, piece(k)]
        return remote(spot, spot, d_send.at[way, at], d_recv.at[way, at, k], to(way))

    def meta_arrived(way, at):
        return remote(mb.at[way, at], mb.at[way, at], m_send.at[way, at], m_recv.at[way, at], to(way))

    def own_meta(way):
        return remote(meta_ref, mb.at[way, 0], m_send.at[way, 0], m_recv.at[way, 0], to(way))

    def meta_copy(way, at):
        return remote(mb.at[way, at], mb.at[way, at + 1], m_send.at[way, at + 1], m_recv.at[way, at + 1], to(way))

    def pack_copy(way, half):
        lanes = pl.ds(half * PACK // 2, PACK // 2)
        return remote(pq.at[way, lanes], pin.at[way, lanes], q_send.at[way, half], q_recv.at[way, half], to(way))

    def last_copy(way):
        return remote(
            pin.at[way, pl.ds(PACK // 2, PACK // 2)],
            xb.at[way, pairs - 1, pl.ds(2 * SLOTS + way * SLOTS, SLOTS)],
            f_send.at[way], f_recv.at[way], to(way),
        )

    def last_back(way):
        return remote(rc.at[far - 1, way, pl.ds(way * SLOTS, SLOTS)], r16.at[way], e_send.at[way], e_recv.at[way], to(1 - way))

    def pack_back(way, half):
        lanes = pl.ds(half * PACK // 2, PACK // 2)
        return remote(rq.at[way, lanes], rp.at[way, lanes], g_send.at[way, half], g_recv.at[way, half], to(1 - way))

    def sum_copy(way, step, k):
        return remote(
            rb.at[way, step, piece(k)], rb.at[way, step + 1, piece(k)], a_send.at[way, step], a_recv.at[way, step + 1, k],
            to(1 - way),
        )

    d_part, f_part = win_ref.shape[1], wout_ref.shape[2]
    shards = (win_ref.at[0], wout_ref.at[0], sin_ref, sout_ref)

    def region(a, shard):
        if a % 2 == 0:
            where = pl.ds(shard * d_part, d_part)
            return win.at[core, where, :] if a == 0 else sin.at[where, :]
        where = pl.ds(pl.multiple_of(shard * f_part, 128), f_part)
        return wout.at[core, :, where] if a == 1 else sout.at[:, where]

    def shard_at(a, k):
        return lax.rem(xi + dp - k, dp) if a % 2 == 0 else lax.rem(xi + k, dp)

    def weight_copy(a, k):
        spot = region(a, shard_at(a, k))
        return remote(
            shards[a] if k == 0 else spot, spot, w_send.at[a, k], w_recv.at[a, k], {"dp": x_up if a % 2 == 0 else x_down}
        )

    def twin_copy(a, k):
        spot = region(a, shard_at(a, k))
        return remote(shards[a] if k == 0 else spot, spot, p_send.at[a, k], p_recv.at[a, k], {"expert": partner})

    def twin_wait(a, k):
        shard = shard_at(a, k)
        if a == 0:
            spot = win.at[1 - core, pl.ds(shard * d_part, d_part), :]
        else:
            spot = wout.at[1 - core, :, pl.ds(pl.multiple_of(shard * f_part, 128), f_part)]
        return remote(spot, spot, p_send.at[a, k], p_recv.at[a, k], {"expert": partner})

    def local_copy(a):
        return pltpu.make_async_copy(shards[a], region(a, xi), w_loc.at[a])

    def norm(k):
        for half in range(part // 16):
            at_rows = pl.ds(k * part + half * 16, 16)
            values = tok_ref[at_rows, :].astype(jnp.float32)
            center = values - jnp.mean(values, axis=-1, keepdims=True)
            spread = jnp.mean(center * center, axis=-1, keepdims=True)
            nb[at_rows, :] = (center * lax.rsqrt(spread + 1e-06)).astype(jnp.bfloat16)

    norm(0)
    norm(1)
    pl.semaphore_wait(barrier, 5)
    for a in (0, 1):
        weight_copy(a, 0).start()

    @pl.when(core > 0)
    def _():
        pl.semaphore_wait(go, 1)

    for way in (0, 1):
        own_meta(way).start()
    for k in range(CHUNKS):
        for way in (0, 1):
            own_copy(way, k).start()
        if k + 2 < CHUNKS:
            norm(k + 2)
    for a in range(4):
        local_copy(a).start()
    for a in (0, 1):
        twin_copy(a, 0).start()

    def places(meta, experts):
        meta = meta.astype(jnp.float32)
        ids, gates = meta[0:8], meta[8:16]
        match, gate = [], []
        for expert in experts:
            hit = ids == expert.astype(jnp.float32)
            match.append(jnp.sum(jnp.where(hit, 1.0, 0.0), axis=0, keepdims=True))
            gate.append(jnp.sum(jnp.where(hit, gates, 0.0), axis=0, keepdims=True))
        both = jnp.concatenate([jnp.broadcast_to(m, (8, rows)) for m in match], axis=0)
        before = lax.broadcasted_iota(jnp.int32, (rows, rows), 0) < lax.broadcasted_iota(jnp.int32, (rows, rows), 1)
        earlier = jnp.dot(
            both.astype(jnp.bfloat16),
            jnp.where(before, 1.0, 0.0).astype(jnp.bfloat16),
            preferred_element_type=jnp.float32,
        )
        slot = jnp.where(both > 0.5, earlier, -1.0)
        return [slot[8 * i : 8 * i + 8] for i in range(len(experts))], gate

    def row_of(count):
        return lax.broadcasted_iota(jnp.int32, (count, rows), 0).astype(jnp.float32)

    def choose(meta):
        slot, gate = places(meta, (chip * CORES, chip * CORES + 1))
        pick, spread = [], []
        for i in (0, 1):
            here = jnp.concatenate([slot[i]] * (SLOTS // 8), axis=0) == row_of(SLOTS)
            pick.append(jnp.where(here, 1.0, 0.0))
            spread.append(jnp.where(here, jnp.broadcast_to(gate[i], (SLOTS, rows)), 0.0))
        return jnp.concatenate(pick, axis=0).astype(jnp.bfloat16), jnp.concatenate(spread, axis=0).T.astype(jnp.bfloat16)

    def unit_rows(at, way):
        return pl.ds(pl.multiple_of(lax.rem(at, 2) * 2 * SLOTS + way * SLOTS, SLOTS), SLOTS)

    def gather(way, at):
        picked, st[way, at] = choose(mb[way, at])
        for n in range(width // TILE):
            cols = pl.ds(n * TILE, TILE)
            got = jnp.dot(picked, db[way, at, :, cols], preferred_element_type=jnp.float32).astype(jnp.bfloat16)
            for e in (0, 1):
                xb[e, at // 2, unit_rows(at, way), cols] = got[e * SLOTS : e * SLOTS + SLOTS]

    def gather_own():
        picked, spread = choose(meta_ref[...])
        sp[2] = spread
        for n in range(width // TILE):
            cols = pl.ds(n * TILE, TILE)
            got = jnp.dot(picked, nb[:, cols], preferred_element_type=jnp.float32).astype(jnp.bfloat16)
            for e in (0, 1):
                xb[e, pairs - 1, pl.ds(2 * SLOTS + (1 - e) * SLOTS, SLOTS), cols] = got[e * SLOTS : e * SLOTS + SLOTS]

    def pack(way):
        ahead = 1 - 2 * way
        near = lax.rem(chip + chips + ahead, chips) * CORES
        last = lax.rem(chip + chips + 2 * ahead, chips) * CORES + way
        meta = mb[way, full - 1]
        slot, gate = places(meta, (near, near + 1))
        slot_last, gate_last = places(meta, (last, last))
        slot, gate = slot + slot_last[:1], gate + gate_last[:1]
        slot = [jnp.concatenate([s, s], axis=0) for s in slot]
        row = row_of(16)
        pick, spread = [], []
        for s, g in zip(slot, gate):
            pick.append(jnp.where(s == row, 1.0, 0.0))
            spread.append(jnp.where(s == row, jnp.broadcast_to(g, (16, rows)), 0.0))
        tail_pick, tail_spread = jnp.zeros((16, rows), jnp.float32), jnp.zeros((16, rows), jnp.float32)
        for i, (s, g) in enumerate(zip(slot, gate)):
            inside = jnp.where((row >= 4 * i) & (row < 4 * i + 4), row + (16 - 4 * i), -2.0)
            tail_pick = jnp.where(s == inside, 1.0, tail_pick)
            tail_spread = jnp.where(s == inside, jnp.broadcast_to(g, (16, rows)), tail_spread)
        picked = jnp.concatenate(pick + [tail_pick], axis=0).astype(jnp.bfloat16)
        sp[way] = jnp.concatenate(spread + [tail_spread], axis=0).T.astype(jnp.bfloat16)
        for n in range(width // TILE):
            cols = pl.ds(n * TILE, TILE)
            pq[way, :, cols] = jnp.dot(
                picked, db[way, full - 1, :, cols], preferred_element_type=jnp.float32
            ).astype(jnp.bfloat16)

    def two_dots(source, first, second, store):
        for n in range(hidden // TILE):
            cols = pl.ds(n * TILE, TILE)
            pre = jnp.dot(source(), first(cols), preferred_element_type=jnp.float32)
            hb[:, cols] = jax.nn.gelu(pre, approximate=True).astype(jnp.bfloat16)
        for n in range(width // TILE):
            cols = pl.ds(n * TILE, TILE)
            store(cols, jnp.dot(hb[...], second(cols), preferred_element_type=jnp.float32))

    def ffn(call):
        pair, e = call // 2, lax.rem(call, 2)

        def store(cols, result):
            result = result.astype(jnp.bfloat16)
            for h in (0, 1):
                for way in (0, 1):
                    lo = (2 * h + way) * SLOTS
                    rc[2 * pair + h, way, pl.ds(pl.multiple_of(e * SLOTS, SLOTS), SLOTS), cols] = result[lo : lo + SLOTS]

        two_dots(lambda: xb[e, pair], lambda cols: win[e, :, cols], lambda cols: wout[e, :, cols], store)

    def shared_ffn():
        def store(cols, result):
            base[:, cols] = tok_ref[:, cols].astype(jnp.float32) + result

        two_dots(lambda: nb[...], lambda cols: sin[:, cols], lambda cols: sout[:, cols], store)

    def calls_by(step_index):
        done = jnp.minimum(2 * (step_index // 2), 2 * (step_index + 1 - FFN_FROM))
        return jnp.maximum(done, 0)

    def dispatch(i, carry):
        lo, hi = calls_by(i - 1), calls_by(i)
        lo = jnp.where(i == 0, 0, lo)
        for k in range(CHUNKS):
            for way in (0, 1):
                arrived(way, i, k).wait_recv()

                @pl.when(i + 1 < full)
                def _():
                    block_copy(way, i, k).start()

                if k == 0:
                    meta_arrived(way, i).wait_recv()

                    @pl.when(i + 1 < full)
                    def _():
                        meta_copy(way, i).start()

            if k == 0:

                @pl.when(i == 0)
                def _():
                    gather_own()

                @pl.when(i > 0)
                def _():
                    gather(0, i - 1)

            if k == 1:

                @pl.when(i > 0)
                def _():
                    gather(1, i - 1)

            if k >= 2:

                @pl.when(lo + (k - 2) < hi)
                def _():
                    ffn(lo + (k - 2))

            if k == 3:

                @pl.when((i == min(STAGGER, full) - 1) & (core == 0))
                def _():
                    pl.semaphore_signal(go, inc=1, device_id={"expert": partner}, device_id_type=MESH)

                for hop in range(dp - 1):
                    for first, pair in ((0, (0, 1)), (2 * dp - 2, (2, 3))):

                        @pl.when(i == min(first + 2 * hop + 1, full - 1))
                        def _():
                            for a in pair:
                                weight_copy(a, hop).wait_recv()
                                if hop + 1 < dp - 1:
                                    weight_copy(a, hop + 1).start()
                                if a < 2:
                                    twin_copy(a, hop + 1).start()
                                if hop == dp - 2:
                                    local_copy(a).wait()
                                    if a < 2:
                                        weight_copy(a + 2, 0).start()
                                        for j in range(dp):
                                            twin_wait(a, j).wait_recv()

        return carry

    lax.fori_loop(0, full, dispatch, 0)
    for way in (0, 1):
        pack(way)
        for half in (1, 0):
            pack_copy(way, half).start()
    for way in (0, 1):
        gather(way, full - 1)
    started = max(0, min(2 * ((full - 1) // 2), 2 * (full - FFN_FROM)))
    rest = list(range(started, 2 * (pairs - 1)))

    def run(calls):
        if calls:

            def body(c, carry):
                ffn(c)
                return carry

            lax.fori_loop(calls[0], calls[-1] + 1, body, 0)

    run(rest[: len(rest) // 2])
    for way in (0, 1):
        pack_copy(way, 1).wait_recv()
        last_copy(way).start()
    for way in (0, 1):
        pack_copy(way, 0).wait_recv()
        for e in (0, 1):
            xb[e, pairs - 1, pl.ds(way * SLOTS, 16), :] = pin[way, pl.ds(e * 16, 16), :]
            xb[e, pairs - 1, pl.ds(way * SLOTS + 16, 16), :] = pin[way, pl.ds(48, 16), :]
    run(rest[len(rest) // 2 :])

    def last_unit(e, carry):
        for way in (0, 1):

            @pl.when(e == way)
            def _():
                last_copy(way).wait_recv()

        ffn(2 * (pairs - 1) + e)
        for way in (0, 1):

            @pl.when(e == way)
            def _():
                last_back(way).start()

        return carry

    lax.fori_loop(0, 2, last_unit, 0)
    tail = lax.broadcasted_iota(jnp.int32, (16, width), 0)
    for way in (0, 1):
        for e in (0, 1):
            rq[way, pl.ds(e * 16, 16), :] = rc[far - 2, way, pl.ds(e * SLOTS, 16), :]
    for way in (0, 1):
        pack_back(way, 0).start()
    for way in (0, 1):
        last_back(way).wait_recv()
        rq[way, pl.ds(32, 16), :] = r16[way, pl.ds(0, 16), :]
        tails = [rc[far - 2, way, pl.ds(e * SLOTS + 16, 16), :].astype(jnp.float32) for e in (0, 1)]
        tails.append(r16[way, pl.ds(16, 16), :].astype(jnp.float32))
        rq[way, pl.ds(48, 16), :] = jnp.where(
            tail < 4, tails[0], jnp.where(tail < 8, tails[1], tails[2])
        ).astype(jnp.bfloat16)
    for way in (0, 1):
        pack_back(way, 1).start()

    def combine(way, at, step, k, first):
        at_rows = piece(k)
        total = jnp.dot(st[way, at, at_rows, :], rc[at, way], preferred_element_type=jnp.float32)
        if first:
            total = total + jnp.dot(sp[way, at_rows, :], rp[way], preferred_element_type=jnp.float32)
        else:
            total = total + rb[way, step, at_rows, :].astype(jnp.float32)
        rb[way, step, at_rows, :] = total.astype(jnp.bfloat16)

    for way in (0, 1):
        for half in (0, 1):
            pack_back(way, half).wait_recv()
    for k in range(CHUNKS):
        for way in (0, 1):
            combine(way, full - 1, 0, k, True)
        for way in (0, 1):
            sum_copy(way, 0, k).start()

    def bring_back(j, carry):
        for k in range(CHUNKS):
            for way in (0, 1):
                sum_copy(way, j - 1, k).wait_recv()
                combine(way, full - 1 - j, j, k, False)
            for way in (0, 1):
                sum_copy(way, j, k).start()
            if k == 2:

                @pl.when(j == min(6, full - 1))
                def _():
                    shared_ffn()

        return carry

    lax.fori_loop(1, full, bring_back, 0)

    for k in range(CHUNKS):
        at_rows = piece(k)
        total = base[at_rows, :]
        for e in (0, 1):
            total = total + jnp.dot(
                sp[2, at_rows, e * SLOTS : (e + 1) * SLOTS],
                rc[far - 1, 1 - e, pl.ds(e * SLOTS, SLOTS), :],
                preferred_element_type=jnp.float32,
            )
        for way in (0, 1):
            sum_copy(way, full - 1, k).wait_recv()
            total = total + rb[way, full, at_rows, :].astype(jnp.float32)
        out_ref[at_rows, :] = total.astype(jnp.bfloat16)

    def whole(ref, sem):
        return pltpu.make_async_copy(ref, ref, sem)

    for way in (0, 1):

        def drain(i, carry):
            whole(db.at[way, i], d_send.at[way, i]).wait()
            whole(mb.at[way, i], m_send.at[way, i]).wait()
            whole(rb.at[way, i], a_send.at[way, i]).wait()
            return carry

        lax.fori_loop(0, full, drain, 0)
        for half in (0, 1):
            pack_copy(way, half).wait_send()
            pack_back(way, half).wait_send()
        last_copy(way).wait_send()
        last_back(way).wait_send()
    for a in range(4):
        for k in range(dp - 1):
            weight_copy(a, k).wait_send()
        if a < 2:
            for k in range(dp):
                twin_copy(a, k).wait_send()


def per_device(mesh, tokens, expert_ids, gate_weights, expert_in, expert_out, shared_in, shared_out):
    rows, width = tokens.shape
    hidden = expert_in.shape[2]
    chips, dp = mesh.shape["expert"] // CORES, mesh.shape["dp"]
    far = chips // 2
    full = far - 2
    meta = jnp.concatenate([expert_ids.astype(jnp.bfloat16).T, gate_weights.astype(jnp.bfloat16).T], axis=0)
    vmem = pl.BlockSpec(memory_space=pltpu.VMEM)
    hbm = pl.BlockSpec(memory_space=pl.ANY)
    b16, f32, dma = jnp.bfloat16, jnp.float32, pltpu.SemaphoreType.DMA
    return pl.pallas_call(
        functools.partial(kernel, chips, dp),
        out_shape=jax.ShapeDtypeStruct((rows, width), b16),
        in_specs=[vmem, vmem, hbm, hbm, hbm, hbm],
        out_specs=vmem,
        scratch_shapes=[
            pltpu.VMEM((rows, width), b16),
            pltpu.VMEM((2, full, rows, width), b16),
            pltpu.VMEM((2, full, 16, rows), b16),
            pltpu.VMEM((2, full, rows, 2 * SLOTS), b16),
            pltpu.VMEM((3, rows, PACK), b16),
            pltpu.VMEM((2, PACK, width), b16),
            pltpu.VMEM((2, PACK, width), b16),
            pltpu.VMEM((2, far // 2, 4 * SLOTS, width), b16),
            pltpu.VMEM((far, 2, 2 * SLOTS, width), b16),
            pltpu.VMEM((2, SLOTS, width), b16),
            pltpu.VMEM((2, PACK, width), b16),
            pltpu.VMEM((2, PACK, width), b16),
            pltpu.VMEM((2, full + 1, rows, width), b16),
            pltpu.VMEM((rows, hidden), b16),
            pltpu.VMEM((rows, width), f32),
            pltpu.VMEM((2, width, hidden), b16),
            pltpu.VMEM((2, hidden, width), b16),
            pltpu.VMEM((width, hidden), b16),
            pltpu.VMEM((hidden, width), b16),
            dma((2, full, CHUNKS)),
            dma((2, full)),
            dma((2, full)),
            dma((2, full)),
            dma((2, 2)),
            dma((2, 2)),
            dma((2,)),
            dma((2,)),
            dma((2,)),
            dma((2,)),
            dma((2, 2)),
            dma((2, 2)),
            dma((2, full + 1, CHUNKS)),
            dma((2, full)),
            dma((4, dp - 1)),
            dma((4, dp - 1)),
            dma((4,)),
            dma((2, dp)),
            dma((2, dp)),
            pltpu.SemaphoreType.REGULAR,
        ],
        compiler_params=pltpu.CompilerParams(
            collective_id=0, has_side_effects=True, vmem_limit_bytes=67043328
        ),
        name="moe_ring",
    )(tokens, meta, expert_in, expert_out, shared_in, shared_out)


def solution(mesh):
    placed = (
        P(("sweep", "expert", "dp"), None),
        P(("sweep", "expert", "dp"), None),
        P(("sweep", "expert", "dp"), None),
        P(("sweep", "expert"), "dp", None),
        P(("sweep", "expert"), None, "dp"),
        P(("sweep", "dp"), None),
        P("sweep", "dp"),
    )
    return jax.shard_map(
        functools.partial(per_device, mesh),
        mesh=mesh,
        in_specs=placed,
        out_specs=P(("sweep", "expert", "dp"), None),
        check_vma=False,
    )
```

time: 982 us -> 320 us (0.33)
  waiting for transfers between devices: 846 us -> 0 us
  Pallas kernels: 0 us -> 316 us
  starting transfers between devices: 55.5 us -> 0 us
  local copies, waits for them, and re-layouts: 38.6 us -> 1.77 us
  matrix products: 16.8 us -> 0 us
  between operations: 13.2 us -> 0.01 us
    all_to_all x2 -> x0, waiting for transfers between devices: 742 us -> none  [the longest x1 422 us: per_device(): lax.all_to_all(run_experts(received, full_in, full_out), 'expert', split_...]
    pallas_call x0 -> x1, Pallas kernels: none -> 316 us  [per_device(): pl.pallas_call(functools.partial(kernel, chips, dp), out_shape=jax.ShapeD...]
    all_gather x4 -> x0, waiting for transfers between devices: 102 us -> none  [the longest x1 51.5 us: per_device(): lax.all_gather(expert_in, 'dp', axis=1, tiled=True)]
    all_to_all x2 -> x0, starting transfers between devices: 54.8 us -> none  [the longest x1 47.4 us: per_device(): lax.all_to_all(outgoing, 'expert', split_axis=0, concat_axis=0, tiled=True)]
    dot_general x2 -> x0, matrix products: 16.8 us -> none  [the longest x1 12.4 us: run_experts(): jnp.einsum('gesf,efd->gesd', hidden, weight_out, preferred_element_type=j...]
    reshape x3 -> x0, local copies, waits for them, and re-layouts: 13.9 us -> none  [the longest x1 6.92 us: per_device(): returned.reshape(expert_total * CAP, model_width)[positions]]
  transfers between devices with their start and end apart: 6 -> 0, of which waited for: 4 -> 0; matrix products, arithmetic and copies ran while one was open for 2% -> 0% of each run, Pallas kernels for 0% -> 0%
where the time goes in v2:
time: 320 us; the launch traced here: 319 us
  Pallas kernels  316 us (99%)
    pallas_call x1, Pallas kernels, per_device(): pl.pallas_call(functools.partial(kernel, chips, dp), out_shape=jax.ShapeD...  316 us

profile of v2, /device:TPU:40, one launch (start us, length us, event | category | flops | bytes accessed | tf_op | source)
XLA Modules:
  0.0 319.4 jit_solution(18189742633089283721)
XLA Ops:
  0.0 0.0 copy-start
  0.0 0.7 convert_bitcast_fusion.1
  0.7 0.0 copy-done
  0.7 0.6 pad_maximum_fusion.meta_ref
  1.3 316.4 %moe_ring.1 = bf16[128,1536]{1,0:T(8,128)(2,1)} custom-call(bf16[128,1536]{1,0:T(8,128)(2,1)} %tok_ref.1, bf16[16,128]{1,0:T(8,128)(2,1)} %pad_maximum_fusion.meta_ref, bf16[1,384,768]{2,1,0:T(8,128)(2,1)} %win_ref.1, bf16[1,768,384]{2,1,0:T(8,128)(2,1)} %wout_ref.1, bf16[384,768]{1,0:T(8,128)(2,1)} %sin_ref.1, bf16[768,384]{1,0:T(8,128)(2,1)} %sout_ref.1), custom_call_target="tpu_custom_call" | custom-call | tf_op jit(solution)/shard_map/moe_ring/pallas_call | solution.py:490
  317.7 1.8 copy.9
  (1 shorter events, 0.0 us)
Async XLA Ops:
  0.0 0.7 copy-start

commit v3 on v2

--- a/solution.py
+++ b/solution.py
@@ -9,20 +9,19 @@
 
 CORES = 2
 SLOTS = 32
-PACK = 64
+NEAR = 48
 CHUNKS = 4
 FFN_FROM = 8
-STAGGER = 3
 TILE = 256
 MESH = pl.DeviceIdType.MESH
 
 
 def kernel(
-    chips, dp, tok_ref, meta_ref, win_ref, wout_ref, sin_ref, sout_ref, out_ref,
-    nb, db, mb, st, sp, pq, pin, xb, rc, r16, rq, rp, rb, hb, base, win, wout, sin, sout,
+    chips, dp, tok_ref, ids_ref, gates_ref, win_ref, wout_ref, sin_ref, sout_ref, out_ref,
+    mo, nb, db, mb, st, sp, so, pq, pin, xb, rc, rq, rp, rb, hb, base, win, wout, sin, sout,
     d_recv, d_send, m_recv, m_send, q_recv, q_send, f_recv, f_send,
     e_recv, e_send, g_recv, g_send, a_recv, a_send,
-    w_recv, w_send, w_loc, p_recv, p_send, go,
+    w_recv, w_send, w_loc, p_recv, p_send,
 ):
     far = chips // 2
     full = far - 2
@@ -39,9 +38,12 @@
     xi = lax.axis_index("dp")
     x_up, x_down = lax.rem(xi + 1, dp), lax.rem(xi + dp - 1, dp)
     towards = (right, left)
+    right2 = lax.rem(chip + 2, chips) * CORES + core
+    left2 = lax.rem(chip + chips - 2, chips) * CORES + core
 
     barrier = pltpu.get_barrier_semaphore()
-    for peer in ({"expert": right}, {"expert": left}, {"expert": partner}, {"dp": x_up}, {"dp": x_down}):
+    peers = [{"expert": p} for p in (right, left, partner, right2, left2)] + [{"dp": x_up}, {"dp": x_down}]
+    for peer in peers:
         pl.semaphore_signal(barrier, inc=1, device_id=peer, device_id_type=MESH)
 
     def remote(source, target, send, recv, device):
@@ -72,28 +74,30 @@
         return remote(mb.at[way, at], mb.at[way, at], m_send.at[way, at], m_recv.at[way, at], to(way))
 
     def own_meta(way):
-        return remote(meta_ref, mb.at[way, 0], m_send.at[way, 0], m_recv.at[way, 0], to(way))
+        return remote(mo, mb.at[way, 0], m_send.at[way, 0], m_recv.at[way, 0], to(way))
 
     def meta_copy(way, at):
         return remote(mb.at[way, at], mb.at[way, at + 1], m_send.at[way, at + 1], m_recv.at[way, at + 1], to(way))
 
-    def pack_copy(way, half):
-        lanes = pl.ds(half * PACK // 2, PACK // 2)
-        return remote(pq.at[way, lanes], pin.at[way, lanes], q_send.at[way, half], q_recv.at[way, half], to(way))
+    def near_copy(way):
+        return remote(pq.at[way, pl.ds(0, NEAR)], pin.at[way], q_send.at[way], q_recv.at[way], to(way))
 
     def last_copy(way):
         return remote(
-            pin.at[way, pl.ds(PACK // 2, PACK // 2)],
-            xb.at[way, pairs - 1, pl.ds(2 * SLOTS + way * SLOTS, SLOTS)],
-            f_send.at[way], f_recv.at[way], to(way),
+            pq.at[way, pl.ds(NEAR, SLOTS)],
+            xb.at[way, pairs - 1, pl.ds(pl.multiple_of(2 * SLOTS + way * SLOTS, SLOTS), SLOTS)],
+            f_send.at[way], f_recv.at[way], {"expert": jnp.where(way == 0, right2, left2)},
         )
 
     def last_back(way):
-        return remote(rc.at[far - 1, way, pl.ds(way * SLOTS, SLOTS)], r16.at[way], e_send.at[way], e_recv.at[way], to(1 - way))
-
-    def pack_back(way, half):
-        lanes = pl.ds(half * PACK // 2, PACK // 2)
-        return remote(rq.at[way, lanes], rp.at[way, lanes], g_send.at[way, half], g_recv.at[way, half], to(1 - way))
+        return remote(
+            rc.at[far - 1, way, pl.ds(pl.multiple_of(way * SLOTS, SLOTS), SLOTS)],
+            rp.at[way, pl.ds(NEAR, SLOTS)],
+            e_send.at[way], e_recv.at[way], {"expert": jnp.where(way == 0, left2, right2)},
+        )
+
+    def near_back(way):
+        return remote(rq.at[way], rp.at[way, pl.ds(0, NEAR)], g_send.at[way], g_recv.at[way], to(1 - way))
 
     def sum_copy(way, step, k):
         return remote(
@@ -143,15 +147,12 @@
             spread = jnp.mean(center * center, axis=-1, keepdims=True)
             nb[at_rows, :] = (center * lax.rsqrt(spread + 1e-06)).astype(jnp.bfloat16)
 
+    mo[...] = jnp.concatenate([ids_ref[...].astype(jnp.float32), gates_ref[...]], axis=0).astype(jnp.bfloat16)
     norm(0)
     norm(1)
-    pl.semaphore_wait(barrier, 5)
+    pl.semaphore_wait(barrier, len(peers))
     for a in (0, 1):
         weight_copy(a, 0).start()
-
-    @pl.when(core > 0)
-    def _():
-        pl.semaphore_wait(go, 1)
 
     for way in (0, 1):
         own_meta(way).start()
@@ -207,8 +208,8 @@
                 xb[e, at // 2, unit_rows(at, way), cols] = got[e * SLOTS : e * SLOTS + SLOTS]
 
     def gather_own():
-        picked, spread = choose(meta_ref[...])
-        sp[2] = spread
+        picked, spread = choose(mo[...])
+        so[...] = spread
         for n in range(width // TILE):
             cols = pl.ds(n * TILE, TILE)
             got = jnp.dot(picked, nb[:, cols], preferred_element_type=jnp.float32).astype(jnp.bfloat16)
@@ -222,34 +223,37 @@
         meta = mb[way, full - 1]
         slot, gate = places(meta, (near, near + 1))
         slot_last, gate_last = places(meta, (last, last))
-        slot, gate = slot + slot_last[:1], gate + gate_last[:1]
-        slot = [jnp.concatenate([s, s], axis=0) for s in slot]
         row = row_of(16)
         pick, spread = [], []
-        for s, g in zip(slot, gate):
-            pick.append(jnp.where(s == row, 1.0, 0.0))
-            spread.append(jnp.where(s == row, jnp.broadcast_to(g, (16, rows)), 0.0))
         tail_pick, tail_spread = jnp.zeros((16, rows), jnp.float32), jnp.zeros((16, rows), jnp.float32)
-        for i, (s, g) in enumerate(zip(slot, gate)):
+        for i in (0, 1):
+            where = jnp.concatenate([slot[i], slot[i]], axis=0)
+            weight = jnp.broadcast_to(gate[i], (16, rows))
+            pick.append(jnp.where(where == row, 1.0, 0.0))
+            spread.append(jnp.where(where == row, weight, 0.0))
             inside = jnp.where((row >= 4 * i) & (row < 4 * i + 4), row + (16 - 4 * i), -2.0)
-            tail_pick = jnp.where(s == inside, 1.0, tail_pick)
-            tail_spread = jnp.where(s == inside, jnp.broadcast_to(g, (16, rows)), tail_spread)
-        picked = jnp.concatenate(pick + [tail_pick], axis=0).astype(jnp.bfloat16)
-        sp[way] = jnp.concatenate(spread + [tail_spread], axis=0).T.astype(jnp.bfloat16)
+            tail_pick = jnp.where(where == inside, 1.0, tail_pick)
+            tail_spread = jnp.where(where == inside, weight, tail_spread)
+        here = jnp.concatenate([slot_last[0]] * (SLOTS // 8), axis=0) == row_of(SLOTS)
+        pick += [tail_pick, jnp.where(here, 1.0, 0.0)]
+        spread += [tail_spread, jnp.where(here, jnp.broadcast_to(gate_last[0], (SLOTS, rows)), 0.0)]
+        picked = jnp.concatenate(pick, axis=0).astype(jnp.bfloat16)
+        filler = [jnp.zeros((rows - NEAR - SLOTS, rows), jnp.float32)]
+        sp[way] = jnp.concatenate(spread + filler, axis=0).T[:, : NEAR + SLOTS].astype(jnp.bfloat16)
         for n in range(width // TILE):
             cols = pl.ds(n * TILE, TILE)
             pq[way, :, cols] = jnp.dot(
                 picked, db[way, full - 1, :, cols], preferred_element_type=jnp.float32
             ).astype(jnp.bfloat16)
 
-    def two_dots(source, first, second, store):
+    def two_dots(count, source, first, second, store):
         for n in range(hidden // TILE):
             cols = pl.ds(n * TILE, TILE)
             pre = jnp.dot(source(), first(cols), preferred_element_type=jnp.float32)
-            hb[:, cols] = jax.nn.gelu(pre, approximate=True).astype(jnp.bfloat16)
+            hb[:count, cols] = jax.nn.gelu(pre, approximate=True).astype(jnp.bfloat16)
         for n in range(width // TILE):
             cols = pl.ds(n * TILE, TILE)
-            store(cols, jnp.dot(hb[...], second(cols), preferred_element_type=jnp.float32))
+            store(cols, jnp.dot(hb[:count], second(cols), preferred_element_type=jnp.float32))
 
     def ffn(call):
         pair, e = call // 2, lax.rem(call, 2)
@@ -261,13 +265,26 @@
                     lo = (2 * h + way) * SLOTS
                     rc[2 * pair + h, way, pl.ds(pl.multiple_of(e * SLOTS, SLOTS), SLOTS), cols] = result[lo : lo + SLOTS]
 
-        two_dots(lambda: xb[e, pair], lambda cols: win[e, :, cols], lambda cols: wout[e, :, cols], store)
+        two_dots(4 * SLOTS, lambda: xb[e, pair], lambda cols: win[e, :, cols], lambda cols: wout[e, :, cols], store)
+
+    def ffn_one(h, e):
+        def store(cols, result):
+            result = result.astype(jnp.bfloat16)
+            for way in (0, 1):
+                rc[far - 2 + h, way, pl.ds(pl.multiple_of(e * SLOTS, SLOTS), SLOTS), cols] = result[
+                    way * SLOTS : (way + 1) * SLOTS
+                ]
+
+        source = pl.ds(2 * SLOTS * h, 2 * SLOTS)
+        two_dots(
+            2 * SLOTS, lambda: xb[e, pairs - 1, source, :], lambda cols: win[e, :, cols], lambda cols: wout[e, :, cols], store
+        )
 
     def shared_ffn():
         def store(cols, result):
             base[:, cols] = tok_ref[:, cols].astype(jnp.float32) + result
 
-        two_dots(lambda: nb[...], lambda cols: sin[:, cols], lambda cols: sout[:, cols], store)
+        two_dots(rows, lambda: nb[...], lambda cols: sin[:, cols], lambda cols: sout[:, cols], store)
 
     def calls_by(step_index):
         done = jnp.minimum(2 * (step_index // 2), 2 * (step_index + 1 - FFN_FROM))
@@ -314,10 +331,6 @@
                     ffn(lo + (k - 2))
 
             if k == 3:
-
-                @pl.when((i == min(STAGGER, full) - 1) & (core == 0))
-                def _():
-                    pl.semaphore_signal(go, inc=1, device_id={"expert": partner}, device_id_type=MESH)
 
                 for hop in range(dp - 1):
                     for first, pair in ((0, (0, 1)), (2 * dp - 2, (2, 3))):
@@ -342,8 +355,9 @@
     lax.fori_loop(0, full, dispatch, 0)
     for way in (0, 1):
         pack(way)
-        for half in (1, 0):
-            pack_copy(way, half).start()
+    for way in (0, 1):
+        last_copy(way).start()
+        near_copy(way).start()
     for way in (0, 1):
         gather(way, full - 1)
     started = max(0, min(2 * ((full - 1) // 2), 2 * (full - FFN_FROM)))
@@ -359,49 +373,35 @@
             lax.fori_loop(calls[0], calls[-1] + 1, body, 0)
 
     run(rest[: len(rest) // 2])
-    for way in (0, 1):
-        pack_copy(way, 1).wait_recv()
-        last_copy(way).start()
-    for way in (0, 1):
-        pack_copy(way, 0).wait_recv()
+
+    def last_unit(e, carry):
+        last_copy(e).wait_recv()
+        ffn_one(1, e)
+        last_back(e).start()
+        return carry
+
+    lax.fori_loop(0, 2, last_unit, 0)
+    for way in (0, 1):
+        near_copy(way).wait_recv()
         for e in (0, 1):
             xb[e, pairs - 1, pl.ds(way * SLOTS, 16), :] = pin[way, pl.ds(e * 16, 16), :]
-            xb[e, pairs - 1, pl.ds(way * SLOTS + 16, 16), :] = pin[way, pl.ds(48, 16), :]
-    run(rest[len(rest) // 2 :])
-
-    def last_unit(e, carry):
-        for way in (0, 1):
-
-            @pl.when(e == way)
-            def _():
-                last_copy(way).wait_recv()
-
-        ffn(2 * (pairs - 1) + e)
-        for way in (0, 1):
-
-            @pl.when(e == way)
-            def _():
-                last_back(way).start()
-
+            xb[e, pairs - 1, pl.ds(way * SLOTS + 16, 16), :] = pin[way, pl.ds(32, 16), :]
+
+    def near_unit(e, carry):
+        ffn_one(0, e)
         return carry
 
-    lax.fori_loop(0, 2, last_unit, 0)
+    lax.fori_loop(0, 2, near_unit, 0)
     tail = lax.broadcasted_iota(jnp.int32, (16, width), 0)
     for way in (0, 1):
+        tails = []
         for e in (0, 1):
             rq[way, pl.ds(e * 16, 16), :] = rc[far - 2, way, pl.ds(e * SLOTS, 16), :]
-    for way in (0, 1):
-        pack_back(way, 0).start()
-    for way in (0, 1):
-        last_back(way).wait_recv()
-        rq[way, pl.ds(32, 16), :] = r16[way, pl.ds(0, 16), :]
-        tails = [rc[far - 2, way, pl.ds(e * SLOTS + 16, 16), :].astype(jnp.float32) for e in (0, 1)]
-        tails.append(r16[way, pl.ds(16, 16), :].astype(jnp.float32))
-        rq[way, pl.ds(48, 16), :] = jnp.where(
-            tail < 4, tails[0], jnp.where(tail < 8, tails[1], tails[2])
-        ).astype(jnp.bfloat16)
-    for way in (0, 1):
-        pack_back(way, 1).start()
+            tails.append(rc[far - 2, way, pl.ds(e * SLOTS + 16, 16), :].astype(jnp.float32))
+        rq[way, pl.ds(32, 16), :] = jnp.where(tail < 4, tails[0], tails[1]).astype(jnp.bfloat16)
+    for way in (0, 1):
+        near_back(way).start()
+    run(rest[len(rest) // 2 :])
 
     def combine(way, at, step, k, first):
         at_rows = piece(k)
@@ -413,8 +413,8 @@
         rb[way, step, at_rows, :] = total.astype(jnp.bfloat16)
 
     for way in (0, 1):
-        for half in (0, 1):
-            pack_back(way, half).wait_recv()
+        last_back(way).wait_recv()
+        near_back(way).wait_recv()
     for k in range(CHUNKS):
         for way in (0, 1):
             combine(way, full - 1, 0, k, True)
@@ -443,7 +443,7 @@
         total = base[at_rows, :]
         for e in (0, 1):
             total = total + jnp.dot(
-                sp[2, at_rows, e * SLOTS : (e + 1) * SLOTS],
+                so[at_rows, e * SLOTS : (e + 1) * SLOTS],
                 rc[far - 1, 1 - e, pl.ds(e * SLOTS, SLOTS), :],
                 preferred_element_type=jnp.float32,
             )
@@ -464,9 +464,8 @@
             return carry
 
         lax.fori_loop(0, full, drain, 0)
-        for half in (0, 1):
-            pack_copy(way, half).wait_send()
-            pack_back(way, half).wait_send()
+        near_copy(way).wait_send()
+        near_back(way).wait_send()
         last_copy(way).wait_send()
         last_back(way).wait_send()
     for a in range(4):
@@ -483,28 +482,28 @@
     chips, dp = mesh.shape["expert"] // CORES, mesh.shape["dp"]
     far = chips // 2
     full = far - 2
-    meta = jnp.concatenate([expert_ids.astype(jnp.bfloat16).T, gate_weights.astype(jnp.bfloat16).T], axis=0)
     vmem = pl.BlockSpec(memory_space=pltpu.VMEM)
     hbm = pl.BlockSpec(memory_space=pl.ANY)
     b16, f32, dma = jnp.bfloat16, jnp.float32, pltpu.SemaphoreType.DMA
     return pl.pallas_call(
         functools.partial(kernel, chips, dp),
         out_shape=jax.ShapeDtypeStruct((rows, width), b16),
-        in_specs=[vmem, vmem, hbm, hbm, hbm, hbm],
+        in_specs=[vmem, vmem, vmem, hbm, hbm, hbm, hbm],
         out_specs=vmem,
         scratch_shapes=[
+            pltpu.VMEM((16, rows), b16),
             pltpu.VMEM((rows, width), b16),
             pltpu.VMEM((2, full, rows, width), b16),
             pltpu.VMEM((2, full, 16, rows), b16),
             pltpu.VMEM((2, full, rows, 2 * SLOTS), b16),
-            pltpu.VMEM((3, rows, PACK), b16),
-            pltpu.VMEM((2, PACK, width), b16),
-            pltpu.VMEM((2, PACK, width), b16),
+            pltpu.VMEM((2, rows, NEAR + SLOTS), b16),
+            pltpu.VMEM((rows, 2 * SLOTS), b16),
+            pltpu.VMEM((2, NEAR + SLOTS, width), b16),
+            pltpu.VMEM((2, NEAR, width), b16),
             pltpu.VMEM((2, far // 2, 4 * SLOTS, width), b16),
             pltpu.VMEM((far, 2, 2 * SLOTS, width), b16),
-            pltpu.VMEM((2, SLOTS, width), b16),
-            pltpu.VMEM((2, PACK, width), b16),
-            pltpu.VMEM((2, PACK, width), b16),
+            pltpu.VMEM((2, NEAR, width), b16),
+            pltpu.VMEM((2, NEAR + SLOTS, width), b16),
             pltpu.VMEM((2, full + 1, rows, width), b16),
             pltpu.VMEM((rows, hidden), b16),
             pltpu.VMEM((rows, width), f32),
@@ -516,14 +515,14 @@
             dma((2, full)),
             dma((2, full)),
             dma((2, full)),
-            dma((2, 2)),
-            dma((2, 2)),
-            dma((2,)),
-            dma((2,)),
-            dma((2,)),
-            dma((2,)),
-            dma((2, 2)),
-            dma((2, 2)),
+            dma((2,)),
+            dma((2,)),
+            dma((2,)),
+            dma((2,)),
+            dma((2,)),
+            dma((2,)),
+            dma((2,)),
+            dma((2,)),
             dma((2, full + 1, CHUNKS)),
             dma((2, full)),
             dma((4, dp - 1)),
@@ -531,13 +530,12 @@
             dma((4,)),
             dma((2, dp)),
             dma((2, dp)),
-            pltpu.SemaphoreType.REGULAR,
         ],
         compiler_params=pltpu.CompilerParams(
             collective_id=0, has_side_effects=True, vmem_limit_bytes=67043328
         ),
         name="moe_ring",
-    )(tokens, meta, expert_in, expert_out, shared_in, shared_out)
+    )(tokens, expert_ids.T, gate_weights.T, expert_in, expert_out, shared_in, shared_out)
 
 
 def solution(mesh):

time: 320 us -> 311 us (0.972)
  Pallas kernels: 316 us -> 309 us
    pallas_call x1, Pallas kernels: 316 us -> 309 us  [per_device(): pl.pallas_call(functools.partial(kernel, chips, dp), out_shape=jax.ShapeD...]
where the time goes in v3:
time: 311 us
  Pallas kernels  309 us (99%)
    pallas_call x1, Pallas kernels, per_device(): pl.pallas_call(functools.partial(kernel, chips, dp), out_shape=jax.ShapeD...  309 us

profile of v3, /device:TPU:40, one launch (start us, length us, event | category | flops | bytes accessed | tf_op | source)
XLA Modules:
  0.0 311.2 jit_solution(12735230096266193253)
XLA Ops:
  0.0 309.4 %moe_ring.1 = bf16[128,1536]{1,0:T(8,128)(2,1)} custom-call(bf16[128,1536]{1,0:T(8,128)(2,1)} %tok_ref.1, s32[8,128]{1,0:T(8,128)} %bitcast.2, f32[8,128]{1,0:T(8,128)} %bitcast.3, bf16[1,384,768]{2,1,0:T(8,128)(2,1)} %win_ref.1, bf16[1,768,384]{2,1,0:T(8,128)(2,1)} %wout_ref.1, bf16[384,768]{1,0:T(8,128)(2,1)} %sin_ref.1, bf16[768,384]{1,0:T(8,128)(2,1)} %sout_ref.1), custom_call_target="tpu_custom_call" | custom-call | tf_op jit(solution)/shard_map/moe_ring/pallas_call | solution.py:488
  309.4 1.8 copy.9

commit v4 on v3

--- a/solution.py
+++ b/solution.py
@@ -18,17 +18,16 @@
 
 def kernel(
     chips, dp, tok_ref, ids_ref, gates_ref, win_ref, wout_ref, sin_ref, sout_ref, out_ref,
-    mo, nb, db, mb, st, sp, so, pq, pin, xb, rc, rq, rp, rb, hb, base, win, wout, sin, sout,
+    tk, ob, mo, nb, db, mb, st, sp, so, ps, pq, pin, xb, rc, rq, rp, rb, hb, base, win, wout, sin, sout,
     d_recv, d_send, m_recv, m_send, q_recv, q_send, f_recv, f_send,
     e_recv, e_send, g_recv, g_send, a_recv, a_send,
-    w_recv, w_send, w_loc, p_recv, p_send,
+    w_recv, w_send, w_loc, p_recv, p_send, t_sem, o_sem,
 ):
     far = chips // 2
     full = far - 2
     pairs = far // 2
-    rows, width = tok_ref.shape
+    rows, width = tk.shape
     hidden = win.shape[2]
-    part = rows // CHUNKS
     me = lax.axis_index("expert")
     core = lax.rem(me, CORES)
     chip = me // CORES
@@ -42,6 +41,19 @@
     left2 = lax.rem(chip + chips - 2, chips) * CORES + core
 
     barrier = pltpu.get_barrier_semaphore()
+    part = rows // CHUNKS
+
+    def piece(k):
+        return pl.ds(k * part, part)
+
+    def token_copy(k):
+        return pltpu.make_async_copy(tok_ref.at[piece(k)], tk.at[piece(k)], t_sem.at[k])
+
+    def out_copy(k):
+        return pltpu.make_async_copy(ob.at[piece(k)], out_ref.at[piece(k)], o_sem.at[k])
+
+    for k in range(CHUNKS):
+        token_copy(k).start()
     peers = [{"expert": p} for p in (right, left, partner, right2, left2)] + [{"dp": x_up}, {"dp": x_down}]
     for peer in peers:
         pl.semaphore_signal(barrier, inc=1, device_id=peer, device_id_type=MESH)
@@ -54,9 +66,6 @@
 
     def to(way):
         return {"expert": towards[way]}
-
-    def piece(k):
-        return pl.ds(k * part, part)
 
     def own_copy(way, k):
         return remote(nb.at[piece(k)], db.at[way, 0, piece(k)], d_send.at[way, 0], d_recv.at[way, 0, k], to(way))
@@ -140,9 +149,10 @@
         return pltpu.make_async_copy(shards[a], region(a, xi), w_loc.at[a])
 
     def norm(k):
+        token_copy(k).wait()
         for half in range(part // 16):
             at_rows = pl.ds(k * part + half * 16, 16)
-            values = tok_ref[at_rows, :].astype(jnp.float32)
+            values = tk[at_rows, :].astype(jnp.float32)
             center = values - jnp.mean(values, axis=-1, keepdims=True)
             spread = jnp.mean(center * center, axis=-1, keepdims=True)
             nb[at_rows, :] = (center * lax.rsqrt(spread + 1e-06)).astype(jnp.bfloat16)
@@ -216,7 +226,7 @@
             for e in (0, 1):
                 xb[e, pairs - 1, pl.ds(2 * SLOTS + (1 - e) * SLOTS, SLOTS), cols] = got[e * SLOTS : e * SLOTS + SLOTS]
 
-    def pack(way):
+    def pack_choice(way):
         ahead = 1 - 2 * way
         near = lax.rem(chip + chips + ahead, chips) * CORES
         last = lax.rem(chip + chips + 2 * ahead, chips) * CORES + way
@@ -237,13 +247,15 @@
         here = jnp.concatenate([slot_last[0]] * (SLOTS // 8), axis=0) == row_of(SLOTS)
         pick += [tail_pick, jnp.where(here, 1.0, 0.0)]
         spread += [tail_spread, jnp.where(here, jnp.broadcast_to(gate_last[0], (SLOTS, rows)), 0.0)]
-        picked = jnp.concatenate(pick, axis=0).astype(jnp.bfloat16)
+        ps[way] = jnp.concatenate(pick, axis=0).astype(jnp.bfloat16)
         filler = [jnp.zeros((rows - NEAR - SLOTS, rows), jnp.float32)]
         sp[way] = jnp.concatenate(spread + filler, axis=0).T[:, : NEAR + SLOTS].astype(jnp.bfloat16)
+
+    def pack(way):
         for n in range(width // TILE):
             cols = pl.ds(n * TILE, TILE)
             pq[way, :, cols] = jnp.dot(
-                picked, db[way, full - 1, :, cols], preferred_element_type=jnp.float32
+                ps[way], db[way, full - 1, :, cols], preferred_element_type=jnp.float32
             ).astype(jnp.bfloat16)
 
     def two_dots(count, source, first, second, store):
@@ -282,7 +294,7 @@
 
     def shared_ffn():
         def store(cols, result):
-            base[:, cols] = tok_ref[:, cols].astype(jnp.float32) + result
+            base[:, cols] = tk[:, cols].astype(jnp.float32) + result
 
         two_dots(rows, lambda: nb[...], lambda cols: sin[:, cols], lambda cols: sout[:, cols], store)
 
@@ -323,6 +335,13 @@
                 @pl.when(i > 0)
                 def _():
                     gather(1, i - 1)
+
+            if k == 2:
+
+                @pl.when(i == full - 1)
+                def _():
+                    pack_choice(0)
+                    pack_choice(1)
 
             if k >= 2:
 
@@ -450,8 +469,11 @@
         for way in (0, 1):
             sum_copy(way, full - 1, k).wait_recv()
             total = total + rb[way, full, at_rows, :].astype(jnp.float32)
-        out_ref[at_rows, :] = total.astype(jnp.bfloat16)
-
+        ob[at_rows, :] = total.astype(jnp.bfloat16)
+        out_copy(k).start()
+
+    for k in range(CHUNKS):
+        out_copy(k).wait()
     def whole(ref, sem):
         return pltpu.make_async_copy(ref, ref, sem)
 
@@ -488,9 +510,11 @@
     return pl.pallas_call(
         functools.partial(kernel, chips, dp),
         out_shape=jax.ShapeDtypeStruct((rows, width), b16),
-        in_specs=[vmem, vmem, vmem, hbm, hbm, hbm, hbm],
-        out_specs=vmem,
+        in_specs=[hbm, vmem, vmem, hbm, hbm, hbm, hbm],
+        out_specs=hbm,
         scratch_shapes=[
+            pltpu.VMEM((rows, width), b16),
+            pltpu.VMEM((rows, width), b16),
             pltpu.VMEM((16, rows), b16),
             pltpu.VMEM((rows, width), b16),
             pltpu.VMEM((2, full, rows, width), b16),
@@ -498,6 +522,7 @@
             pltpu.VMEM((2, full, rows, 2 * SLOTS), b16),
             pltpu.VMEM((2, rows, NEAR + SLOTS), b16),
             pltpu.VMEM((rows, 2 * SLOTS), b16),
+            pltpu.VMEM((2, NEAR + SLOTS, rows), b16),
             pltpu.VMEM((2, NEAR + SLOTS, width), b16),
             pltpu.VMEM((2, NEAR, width), b16),
             pltpu.VMEM((2, far // 2, 4 * SLOTS, width), b16),
@@ -530,6 +555,8 @@
             dma((4,)),
             dma((2, dp)),
             dma((2, dp)),
+            dma((CHUNKS,)),
+            dma((CHUNKS,)),
         ],
         compiler_params=pltpu.CompilerParams(
             collective_id=0, has_side_effects=True, vmem_limit_bytes=67043328

time: 311 us -> 311 us (level)
  no operation moved by 1% of the time
where the time goes in v4:
time: 311 us
  Pallas kernels  309 us (99%)
    pallas_call x1, Pallas kernels, per_device(): pl.pallas_call(functools.partial(kernel, chips, dp), out_shape=jax.ShapeD...  309 us

profile of v4, /device:TPU:40, one launch (start us, length us, event | category | flops | bytes accessed | tf_op | source)
XLA Modules:
  0.0 310.7 jit_solution(12652745644600018044)
XLA Ops:
  0.0 308.9 %moe_ring.1 = bf16[128,1536]{1,0:T(8,128)(2,1)} custom-call(bf16[128,1536]{1,0:T(8,128)(2,1)} %tok_ref.1, s32[8,128]{1,0:T(8,128)} %bitcast.2, f32[8,128]{1,0:T(8,128)} %bitcast.3, bf16[1,384,768]{2,1,0:T(8,128)(2,1)} %win_ref.1, bf16[1,768,384]{2,1,0:T(8,128)(2,1)} %wout_ref.1, bf16[384,768]{1,0:T(8,128)(2,1)} %sin_ref.1, bf16[768,384]{1,0:T(8,128)(2,1)} %sout_ref.1), custom_call_target="tpu_custom_call" | custom-call | tf_op jit(solution)/shard_map/moe_ring/pallas_call | solution.py:510
  308.9 1.8 copy.9
